TPU v7x, 32 devices: a whole 2x2x4 slice. The times are simulated.
32 devices in a mesh: pole: 2 (over y), leaf: 16 (over z, x, core).
Axes of the slice: x: 2, y: 2, z: 4, core: 2. Of those that a mesh axis runs over, the one named last changes fastest.
Arguments:
- root_frame: float32 [2048, 1024], P(('pole', 'leaf')), parts along dimension 0, may hold values from -2 to 8, as said below
- top_lhat: float32 [3072, 256], P(('pole', 'leaf')), parts along dimension 0, may hold values from -0.21875 to 0.21875
- top_dinv: float32 [1024, 256], P(('pole', 'leaf')), parts along dimension 0, may hold values from -2 to 8, as said below
- mid_lhat: float32 [32, 768, 256], P(('pole', 'leaf')), parts along dimension 0, may hold values from -0.21875 to 0.21875
- mid_dinv: float32 [32, 256, 256], P(('pole', 'leaf')), parts along dimension 0, may hold values from -2 to 8, as said below
- leaf_lhat: float32 [64, 768, 256], P(('pole', 'leaf')), parts along dimension 0, may hold values from -0.21875 to 0.21875
- leaf_dinv: float32 [64, 256, 256], P(('pole', 'leaf')), parts along dimension 0, may hold values from -2 to 8, as said below
- top_columns: int32 [2], replicated, may hold values from 128 to 256
- mid_columns: int32 [16], replicated, may hold values from 128 to 256
- leaf_columns: int32 [32], replicated, may hold values from 128 to 256
- top_pattern: int32 [2, 3], replicated, may hold values from 0 to 3, as said below
- mid_parent: int32 [16], replicated, may hold values from 0 to 1, as said below
- leaf_parent: int32 [32], replicated, may hold values from 0 to 15, as said below
- mid_pattern: int32 [16, 3], replicated, may hold values from 0 to 3, as said below
- leaf_pattern: int32 [32, 3], replicated, may hold values from 0 to 3, as said below
- leaf_live: int32 [16], replicated, may hold values from 1 to 2, as said below
Outputs:
- top_diagonal: float32 [1024, 256], P(('pole', 'leaf')), parts along dimension 0
- top_coupling: float32 [3072, 256], P(('pole', 'leaf')), parts along dimension 0
- mid_diagonal: float32 [32, 256, 256], P(('pole', 'leaf')), parts along dimension 0
- mid_coupling: float32 [32, 768, 256], P(('pole', 'leaf')), parts along dimension 0
- leaf_diagonal: float32 [64, 256, 256], P(('pole', 'leaf')), parts along dimension 0
- leaf_coupling: float32 [64, 768, 256], P(('pole', 'leaf')), parts along dimension 0
There are 2 independent parts, one for each index of `pole`. A program takes and returns all parts, laid end to end along the dimension named above; an argument that names none is the same for every part. Nothing has to cross between parts.
Inputs may be any that keep to these rules, and one draw needn't show every extreme that they name: `root_frame`: Symmetric. `top_dinv`: each 256 x 256 block is symmetric. `mid_dinv`: each block is symmetric. `leaf_dinv`: each block is symmetric. `top_pattern`: each row holds 3 distinct increasing numbers of 0 to 3. mid_parent[j] is 2 * (j // 16) plus a number below 2: a level-1 supernode hangs under a level-2 supernode of its own group of 16 devices. leaf_parent[i] is one of the 4 level-1 supernodes numbered from 4 * (i // 8): a leaf hangs under a level-1 supernode of its own group of 4 devices. `mid_pattern`: each row starts with 0 (the parent) and goes on with 2 distinct increasing numbers of 1 to 3. `leaf_pattern`: each row starts with 0 (the parent) and goes on with 2 distinct increasing numbers of 1 to 3. The leaf supernodes of device d are its first leaf_live[d] slots; some device has all 2.
All inputs are finite; a program needn't handle non-finite values.
Results may differ from a plain program's by a relative error of at most 0.0003.
Values sent between devices are 32-bit elements; how exact they have to be, the bound alone decides.
A program may use at most 128 MiB of HBM per device.

v0:
```python
import functools

import jax
import jax.numpy as jnp
from jax import lax
from jax.experimental import pallas as pl
from jax.experimental.pallas import tpu as pltpu
from jax.sharding import PartitionSpec as P

SLOTS = 3
GROUP2 = 16
NODES2 = 2
GROUP1 = 4

MESH = pl.DeviceIdType.MESH
f32 = jnp.float32
bf16 = jnp.bfloat16


def split(value):
    high = value.astype(bf16)
    low = (value - high.astype(f32)).astype(bf16)
    return high, low


def remote(src, dst, send_sem, recv_sem, target):
    return pltpu.make_async_remote_copy(
        src_ref=src,
        dst_ref=dst,
        send_sem=send_sem,
        recv_sem=recv_sem,
        device_id={"leaf": target},
        device_id_type=MESH,
    )


def in_hbm(x):
    return pltpu.with_memory_space_constraint(x, pltpu.HBM)


class Spread:
    def __init__(self, own, whole, group, sems, me, valid=None):
        self.own, self.whole, self.group = own, whole, group
        self.valid = valid
        self.rows = own.shape[0]
        self.recv, self.up, self.down, self.side, self.core, self.local = sems
        self.base = me - lax.rem(me, group)

    def block(self, device):
        start = (device - self.base) * self.rows
        return self.whole.at[pl.ds(pl.multiple_of(start, 8), self.rows)]

    def copy(self, device, target, sems, own=False):
        slot = device - self.base
        return remote(
            self.own if own else self.block(device),
            self.block(device),
            sems.at[slot],
            self.recv.at[slot],
            target,
        )

    def keep(self, me):
        return pltpu.make_async_copy(self.own, self.block(me), self.local.at[0])

    def arrived(self, device, me):
        self.copy(device, me, self.core).wait_recv()


def gather_kernel(
    n,
    pieces,
    root_in,
    tl_in,
    td_in,
    ml_in,
    md_in,
    *rest,
):
    root_alls, rest = rest[:pieces], rest[pieces:]
    tl_all, td_all, ml_all, md_all = rest[:4]
    sems = rest[4:]
    me = lax.axis_index("leaf")
    core = lax.rem(me, 2)
    side = lax.rem(me // 2, 2)
    cpeer = me + 1 - 2 * core
    xpeer = me + 2 - 4 * side
    cols = td_in.shape[1]
    root_rows = root_in.shape[0]
    per = root_in.shape[1] // cols
    block_row = me * root_rows // cols

    def in_half(device):
        return device * root_rows // cols < per // 2

    roots = []
    for k in range(pieces):
        column = pl.multiple_of(lax.rem(block_row + k, per) * cols, cols)
        roots.append(
            Spread(
                root_in.at[:, pl.ds(column, cols)],
                root_alls[k],
                n,
                sems[6 * k : 6 * k + 6],
                me,
                in_half if k == per // 2 else None,
            )
        )
    sems = sems[6 * pieces :]
    tl = Spread(tl_in, tl_all, GROUP2, sems[0:6], me)
    td = Spread(td_in, td_all, GROUP2, sems[6:12], me)
    ml = Spread(ml_in, ml_all, GROUP1, sems[12:18], me)
    md = Spread(md_in, md_all, GROUP1, sems[18:24], me)
    tops = (tl, td)
    mids = (ml, md)

    line = n // GROUP1
    place = me // GROUP1
    top_line = GROUP2 // GROUP1
    top_place = lax.rem(me, GROUP2) // GROUP1
    has_up = place < line - 1
    has_down = place > 0

    barrier = pltpu.get_barrier_semaphore()
    for peer in (cpeer, xpeer):
        pl.semaphore_signal(barrier, inc=1, device_id={"leaf": peer}, device_id_type=MESH)

    @pl.when(has_up)
    def _():
        pl.semaphore_signal(barrier, inc=1, device_id={"leaf": me + GROUP1}, device_id_type=MESH)

    @pl.when(has_down)
    def _():
        pl.semaphore_signal(barrier, inc=1, device_id={"leaf": me - GROUP1}, device_id_type=MESH)

    def when(part, device, act):
        if part.valid is None:
            act()
        else:
            pl.when(part.valid(device))(act)

    for part in tops + mids:
        part.keep(me).start()
    for part in roots:
        when(part, me, lambda: part.keep(me).start())
    peers = 2 + jnp.minimum(place, 1) + jnp.minimum(line - 1 - place, 1)
    pl.semaphore_wait(barrier, peers)

    def along(part, device, go_up, ok, act, own=False):
        if go_up:
            @pl.when(ok)
            def _():
                act(part.copy(device, me + GROUP1, part.up, own))
        else:
            @pl.when(ok)
            def _():
                act(part.copy(device, me - GROUP1, part.down, own))

    def start(copy):
        copy.start()

    def wait_send(copy):
        copy.wait_send()

    top_up = top_place < top_line - 1
    top_down = top_place > 0

    def root_line(device, go_up, act, own=False):
        for part in roots:
            def go():
                along(part, device, go_up, has_up if go_up else has_down, act, own)

            when(part, device, go)

    def root_to(device, target, core_way, act, own=False):
        for part in roots:
            def go():
                act(part.copy(device, target, part.core if core_way else part.side, own))

            when(part, device, go)

    def root_arrived(device):
        for part in roots:
            when(part, device, lambda: part.arrived(device, me))

    def own_copies(act):
        root_to(me, xpeer, False, act, True)
        for part in tops:
            along(part, me, True, top_up, act, True)
            along(part, me, False, top_down, act, True)
        root_line(me, True, act, True)
        root_line(me, False, act, True)
        for part in tops:
            act(part.copy(me, xpeer, part.side, True))
        root_to(me, cpeer, True, act, True)
        for part in tops:
            act(part.copy(me, cpeer, part.core, True))
        for part in mids:
            act(part.copy(me, xpeer, part.side, True))
            act(part.copy(me, cpeer, part.core, True))

    own_copies(start)

    root_arrived(xpeer)
    root_line(xpeer, True, start)
    root_line(xpeer, False, start)
    root_to(xpeer, cpeer, True, start)

    def step(s, carry):
        for go_up in (True, False):
            shift = -s * GROUP1 if go_up else s * GROUP1
            got_top = (top_place >= s) if go_up else (top_place + s < top_line)
            got_root = (place >= s) if go_up else (place + s < line)

            @pl.when(got_top)
            def _():
                for part in tops:
                    part.arrived(me + shift, me)
                    along(part, me + shift, go_up, top_up if go_up else top_down, start)
                    part.copy(me + shift, xpeer, part.side).start()
                    part.copy(me + shift, cpeer, part.core).start()

            @pl.when(got_root)
            def _():
                for device in (me, xpeer):
                    root_arrived(device + shift)
                    root_line(device + shift, go_up, start)
                    root_to(device + shift, cpeer, True, start)

        return carry

    lax.fori_loop(1, line, step, 0)

    for part in tops:
        for q in range(top_line):
            device = part.base + q * GROUP1 + lax.rem(xpeer, GROUP1)
            part.arrived(device, me)
            part.copy(device, cpeer, part.core).start()
    for part in tuple(roots) + tops:
        def other(q, carry):
            for peer in (cpeer, cpeer + xpeer - me):
                device = part.base + q * GROUP1 + lax.rem(peer, GROUP1)
                when(part, device, lambda: part.arrived(device, me))
            return carry

        lax.fori_loop(0, part.group // GROUP1, other, 0)
        when(part, me, lambda: part.keep(me).wait())

    for part in mids:
        part.arrived(xpeer, me)
        part.copy(xpeer, cpeer, part.core).start()
    for part in mids:
        part.arrived(cpeer, me)
        part.arrived(cpeer + xpeer - me, me)
        part.keep(me).wait()

    own_copies(wait_send)
    root_line(xpeer, True, wait_send)
    root_line(xpeer, False, wait_send)
    root_to(xpeer, cpeer, True, wait_send)

    def drain(s, carry):
        for go_up in (True, False):
            shift = -s * GROUP1 if go_up else s * GROUP1
            got_top = (top_place >= s) if go_up else (top_place + s < top_line)
            got_root = (place >= s) if go_up else (place + s < line)

            @pl.when(got_top)
            def _():
                for part in tops:
                    along(part, me + shift, go_up, top_up if go_up else top_down, wait_send)
                    part.copy(me + shift, xpeer, part.side).wait_send()
                    part.copy(me + shift, cpeer, part.core).wait_send()

            @pl.when(got_root)
            def _():
                for device in (me, xpeer):
                    root_line(device + shift, go_up, wait_send)
                    root_to(device + shift, cpeer, True, wait_send)

        return carry

    lax.fori_loop(1, line, drain, 0)
    for part in tops:
        for q in range(top_line):
            device = part.base + q * GROUP1 + lax.rem(xpeer, GROUP1)
            part.copy(device, cpeer, part.core).wait_send()
    for part in mids:
        part.copy(xpeer, cpeer, part.core).wait_send()


def tree_kernel(pieces, *refs):
    small_in, mid_pattern, leaf_pattern = refs[:7], refs[7], refs[8]
    root_alls, refs = refs[9 : 9 + pieces], refs[9 + pieces :]
    tl_all, td_all, ml_all, md_all, leaf_lhat_in, leaf_dinv_in = refs[:6]
    (
        top_diag_out,
        top_coup_out,
        mid_diag_out,
        mid_coup_out,
        leaf_diag_out,
        leaf_coup_out,
    ) = refs[6:12]
    e0h, e0l, e2h, e2l, e1h, e1l, lcat, ccat, top_c, top_d, leaf_lhat, leaf_dinv = refs[12:24]
    small = refs[24:31]
    sems = refs[31]
    top_columns, mid_columns, leaf_columns, top_pattern, mid_parent, leaf_parent, leaf_live = small
    fetched = list(zip(small_in + (leaf_lhat_in, leaf_dinv_in), small + (leaf_lhat, leaf_dinv)))
    fetches = [pltpu.make_async_copy(a, b, sems.at[i]) for i, (a, b) in enumerate(fetched)]
    for fetch in fetches:
        fetch.start()
    me = lax.axis_index("leaf")
    cols = leaf_dinv.shape[2]
    frame = SLOTS * cols

    per = e0h.shape[1]
    for k in range(pieces):
        for a in range(per // 2 if k == per // 2 else per):
            b = (a + k) % per
            value = root_alls[k][a * cols : (a + 1) * cols]
            e0h[0, a, b], e0l[0, a, b] = split(value)
            if k:
                e0h[0, b, a], e0l[0, b, a] = split(value.T)
    for fetch in fetches[:-2]:
        fetch.wait()

    row_ids = lax.broadcasted_iota(jnp.int32, (cols, cols), 0)
    lane_ids = lax.broadcasted_iota(jnp.int32, (cols, cols), 1)

    def solve(src_h, src_l, source, pattern, lhat, dinv, used, put_coup, put_diag, dst=None):
        keep = lane_ids < used
        for r in range(SLOTS):
            high, low = split(jnp.where(keep, lhat(r), 0.0))
            lcat[r * cols : (r + 1) * cols] = high
            lcat[frame + r * cols : frame + (r + 1) * cols] = low
            lcat[2 * frame + r * cols : 2 * frame + (r + 1) * cols] = high
        for r in range(SLOTS):
            highs = [src_h[source, pattern[r], pattern[k]] for k in range(SLOTS)]
            lows = [src_l[source, pattern[r], pattern[k]] for k in range(SLOTS)]
            wide = jnp.concatenate(highs + highs + lows, axis=1)
            coup = -jnp.dot(wide, lcat[...], preferred_element_type=f32)
            put_coup(r, coup)
            high, low = split(coup)
            ccat[r * cols : (r + 1) * cols] = high
            ccat[frame + r * cols : frame + (r + 1) * cols] = high
            ccat[2 * frame + r * cols : 2 * frame + (r + 1) * cols] = low
            if dst is not None:
                dst_h, dst_l, place_at = dst
                dst_h[place_at, r + 1, 0] = high
                dst_l[place_at, r + 1, 0] = low
                high, low = split(coup.T)
                dst_h[place_at, 0, r + 1] = high
                dst_l[place_at, 0, r + 1] = low
                for k in range(SLOTS):
                    dst_h[place_at, r + 1, k + 1] = highs[k]
                    dst_l[place_at, r + 1, k + 1] = lows[k]
        product = lax.dot_general(
            lcat[...], ccat[...], (((0,), (0,)), ((), ())), preferred_element_type=f32
        )
        diag = jnp.where(keep & (row_ids < used), dinv, 0.0) - product
        put_diag(diag)
        if dst is not None:
            high, low = split(diag)
            dst_h[place_at, 0, 0] = high
            dst_l[place_at, 0, 0] = low

    top_base = me // GROUP2 * NODES2

    def top_step(q, carry):
        pattern = [top_pattern[top_base + q, k] for k in range(SLOTS)]

        def lhat(r):
            return tl_all[pl.ds(pl.multiple_of(q * frame + r * cols, cols), cols)]

        def put_coup(r, value):
            top_c[pl.ds(pl.multiple_of(q * frame + r * cols, cols), cols)] = value

        def put_diag(value):
            top_d[pl.ds(pl.multiple_of(q * cols, cols), cols)] = value

        dinv = td_all[pl.ds(pl.multiple_of(q * cols, cols), cols)]
        used = top_columns[top_base + q]
        solve(e0h, e0l, 0, pattern, lhat, dinv, used, put_coup, put_diag, (e2h, e2l, q))
        return carry

    lax.fori_loop(0, NODES2, top_step, 0)
    member = lax.rem(me, GROUP2)
    rows = top_coup_out.shape[0]
    top_coup_out[...] = top_c[pl.ds(pl.multiple_of(member * rows, 8), rows)]
    rows = top_diag_out.shape[0]
    top_diag_out[...] = top_d[pl.ds(pl.multiple_of(member * rows, 8), rows)]

    leaves = leaf_lhat.shape[0]
    mid_base = me // GROUP1 * GROUP1

    def mid_step(step_index, carry):
        k = leaves - step_index
        leaf = me * leaves + jnp.maximum(k - 1, 0)
        local = jnp.where(k == 0, lax.rem(me, GROUP1), leaf_parent[leaf] - mid_base)
        node = mid_base + local
        pattern = [mid_pattern[node, s] for s in range(SLOTS)]

        def lhat(r):
            return ml_all[pl.ds(pl.multiple_of(local * frame + r * cols, cols), cols)]

        def put_coup(r, value):
            mid_coup_out[r * cols : (r + 1) * cols] = value

        def put_diag(value):
            mid_diag_out[...] = value

        dinv = md_all[pl.ds(pl.multiple_of(local * cols, cols), cols)]
        source = mid_parent[node] - top_base
        solve(
            e2h, e2l, source, pattern, lhat, dinv, mid_columns[node], put_coup, put_diag,
            (e1h, e1l, k),
        )
        return carry

    lax.fori_loop(0, leaves + 1, mid_step, 0)

    for fetch in fetches[-2:]:
        fetch.wait()

    def leaf_step(i, carry):
        node = me * leaves + i
        pattern = [leaf_pattern[node, s] for s in range(SLOTS)]
        live = jnp.full((cols, cols), i, jnp.int32) < leaf_live[me]

        def lhat(r):
            return leaf_lhat[i, r * cols : (r + 1) * cols]

        def put_coup(r, value):
            leaf_coup_out[i, r * cols : (r + 1) * cols] = jnp.where(live, value, 0.0)

        def put_diag(value):
            leaf_diag_out[i] = jnp.where(live, value, 0.0)

        solve(e1h, e1l, i + 1, pattern, lhat, leaf_dinv[i], leaf_columns[node], put_coup, put_diag)
        return carry

    lax.fori_loop(0, leaves, leaf_step, 0)


def body(
    root_frame,
    top_lhat,
    top_dinv,
    mid_lhat,
    mid_dinv,
    leaf_lhat,
    leaf_dinv,
    *scalars,
):
    n = lax.axis_size("leaf")
    cols = top_dinv.shape[1]
    frame = SLOTS * cols
    per = root_frame.shape[1] // cols
    leaves = leaf_lhat.shape[0]
    grid = SLOTS + 1

    def dma(count):
        return pltpu.SemaphoreType.DMA((count,))

    pieces = per // 2 + 1
    sems = []
    for group in (n,) * pieces + (GROUP2, GROUP2, GROUP1, GROUP1):
        sems += [dma(group) for _ in range(5)] + [dma(1)]
    vmem = pl.BlockSpec(memory_space=pltpu.VMEM)
    smem = pl.BlockSpec(memory_space=pltpu.SMEM)
    anywhere = pl.BlockSpec(memory_space=pl.ANY)
    mine = (root_frame, top_lhat, top_dinv, mid_lhat[0], mid_dinv[0])
    groups = (GROUP2, GROUP2, GROUP1, GROUP1)
    root_rows = n * root_frame.shape[0]
    root_shapes = [
        jax.ShapeDtypeStruct((root_rows // 2 if k == per // 2 else root_rows, cols), f32)
        for k in range(pieces)
    ]
    hbm = pl.BlockSpec(memory_space=pltpu.HBM)
    whole = pl.pallas_call(
        functools.partial(gather_kernel, n, pieces),
        out_shape=root_shapes
        + [
            jax.ShapeDtypeStruct((count * x.shape[0], x.shape[1]), f32)
            for count, x in zip(groups, mine[1:])
        ],
        in_specs=[hbm] * 5,
        out_specs=[anywhere] * (pieces + 4),
        scratch_shapes=sems,
        compiler_params=pltpu.CompilerParams(
            collective_id=0, has_side_effects=True, vmem_limit_bytes=1024 * 1024
        ),
    )(*[in_hbm(x) for x in mine])
    small = scalars[:6] + scalars[8:]
    outs = pl.pallas_call(
        functools.partial(tree_kernel, pieces),
        out_shape=[
            jax.ShapeDtypeStruct(top_dinv.shape, f32),
            jax.ShapeDtypeStruct(top_lhat.shape, f32),
            jax.ShapeDtypeStruct(mid_dinv.shape[1:], f32),
            jax.ShapeDtypeStruct(mid_lhat.shape[1:], f32),
            jax.ShapeDtypeStruct(leaf_dinv.shape, f32),
            jax.ShapeDtypeStruct(leaf_lhat.shape, f32),
        ],
        in_specs=[hbm] * 7 + [smem] * 2 + [vmem] * (pieces + 4) + [hbm] * 2,
        out_specs=[vmem] * 6,
        scratch_shapes=[
            pltpu.VMEM((1, per, per, cols, cols), bf16),
            pltpu.VMEM((1, per, per, cols, cols), bf16),
            pltpu.VMEM((NODES2, grid, grid, cols, cols), bf16),
            pltpu.VMEM((NODES2, grid, grid, cols, cols), bf16),
            pltpu.VMEM((leaves + 1, grid, grid, cols, cols), bf16),
            pltpu.VMEM((leaves + 1, grid, grid, cols, cols), bf16),
            pltpu.VMEM((3 * frame, cols), bf16),
            pltpu.VMEM((3 * frame, cols), bf16),
            pltpu.VMEM((NODES2 * frame, cols), f32),
            pltpu.VMEM((NODES2 * cols, cols), f32),
            pltpu.VMEM(leaf_lhat.shape, f32),
            pltpu.VMEM(leaf_dinv.shape, f32),
        ]
        + [pltpu.SMEM(x.shape, jnp.int32) for x in small]
        + [dma(len(small) + 2)],
        compiler_params=pltpu.CompilerParams(vmem_limit_bytes=36 * 1024 * 1024),
    )(
        *[in_hbm(x) for x in small], scalars[6], scalars[7], *whole, in_hbm(leaf_lhat), in_hbm(leaf_dinv)
    )
    return (outs[0], outs[1], outs[2][None], outs[3][None], outs[4], outs[5])


def solution(mesh):
    rows = P(("pole", "leaf"), None)
    stacks = P(("pole", "leaf"), None, None)
    in_specs = (rows,) * 3 + (stacks,) * 4 + (P(),) * 9
    out_specs = (rows,) * 2 + (stacks,) * 4
    return jax.shard_map(body, mesh=mesh, in_specs=in_specs, out_specs=out_specs, check_vma=False)
```

profile of v0, /device:TPU:0, one launch (start us, length us, event | category | flops | bytes accessed | tf_op | source)
XLA Modules:
  0.0 71.2 jit_solution(1971482971104572312)
XLA Ops:
  0.6 0.8 %copy.22.refs_7_ = s32[16,3]{1,0:T(8,128)S(1)} copy(s32[16,3]{0,1:T(4,128)} %param.29) | data formatting | bytes 384 | tf_op args[13]
  1.4 0.8 %copy.23.refs_8_ = s32[32,3]{1,0:T(8,128)S(1)} copy(s32[32,3]{0,1:T(4,128)} %param.30) | data formatting | bytes 768 | tf_op args[14]
  2.2 50.8 %shard_map.199 = (f32[1024,256]{1,0:T(8,128)S(1)}, f32[1024,256]{1,0:T(8,128)S(1)}, f32[512,256]{1,0:T(8,128)S(1)}, f32[1536,256]{1,0:T(8,128)S(1)}, f32[512,256...) custom-call(f32[64,1024]{1,0:T(8,128)} %root_in.1, f32[96,256]{1,0:T(8,128)} %tl_in.1, ...), custom_call_target="tpu_custom_call" | custom-call | tf_op jit(solution)/shard_map/pallas_call | solution.py:480
  52.9 18.2 %shard_map.200 = (f32[32,256]{1,0:T(8,128)}, f32[96,256]{1,0:T(8,128)}, f32[256,256]{1,0:T(8,128)}, f32[768,256]{1,0:T(8,128)}, f32[2,256,256]{2,1,0:T(8,128)}, /*index=5*/f32[2,768,256]{2,1,0:T(8,128)}) custom-call(s32[2]{0:T(128)} %refs_0_.1, s32[16]{0:T(128)} %refs_1_.1, s32[32]{0:T(128)} %refs_2_.1, s32[2,3]{1,0:T(2,128)} %refs_3_.1, s32[16]{0:T(128)} %refs_4_.1, ...), custom_call_target="tpu_custom_call" | custom-call | tf_op jit(solution)/shard_map/pallas_call | solution.py:495
where the time goes:
time: 71.4 us; the launch traced here: 71.2 us
  Pallas kernels  69 us (97%)
  local copies, waits for them, and re-layouts  1.52 us (2%)
    pallas_call x1, Pallas kernels, body(): pl.pallas_call(functools.partial(gather_kernel, n, pieces), out_shape=roo...  50.8 us
    pallas_call x1, Pallas kernels, body(): pl.pallas_call(functools.partial(tree_kernel, pieces), out_shape=[jax.Sha...  18.2 us
    unnamed x2, local copies, waits for them, and re-layouts  1.52 us

commit v1 on v0

v1 whole, which is shorter than its diff:
```python
import functools

import jax
import jax.numpy as jnp
from jax import lax
from jax.experimental import pallas as pl
from jax.experimental.pallas import tpu as pltpu
from jax.sharding import PartitionSpec as P

SLOTS = 3
GROUP2 = 16
NODES2 = 2
GROUP1 = 4
TILE = 128
OWN = 2 * SLOTS + 1

MESH = pl.DeviceIdType.MESH
f32 = jnp.float32
bf16 = jnp.bfloat16


def split(value):
    high = value.astype(bf16)
    low = (value - high.astype(f32)).astype(bf16)
    return high, low


def in_hbm(x):
    return pltpu.with_memory_space_constraint(x, pltpu.HBM)


def root_windows(tiles):
    if tiles == 8:
        return [(0, 7), (1, 7), (2, 6), (3, 6), (4, 6), (5, 6), (2, 7), (0, 8)]
    return [(r, tiles) for r in range(tiles)]


def half_windows(tiles):
    return [(r, tiles) for r in range(tiles)]


class Part:
    def __init__(self, own, place, group, sems, me, total, rows=0, windows=None):
        self.own, self.place, self.group, self.total = own, place, group, total
        self.recv, self.recv_core, self.line, self.side, self.core, self.local = sems
        self.base = me - lax.rem(me, group)
        self.rows, self.windows = rows, windows
        self.me = me

    def cases(self, device, act):
        if self.windows is None:
            act(None)
            return
        row = lax.rem(lax.div((device - self.base) * self.rows, TILE), len(self.windows))
        for i, window in enumerate(self.windows):
            pl.when(row == i)(functools.partial(act, window))

    def view(self, ref, window):
        if window is None:
            return ref
        return ref.at[:, window[0] * TILE : window[1] * TILE]

    def copy(self, device, window, target, send, recv, own=False):
        dst = self.view(self.place(device - self.base), window)
        return pltpu.make_async_remote_copy(
            src_ref=self.view(self.own, window) if own else dst,
            dst_ref=dst,
            send_sem=send,
            recv_sem=recv,
            device_id={"leaf": target},
            device_id_type=MESH,
        )

    def slot(self, device):
        return lax.div(device - self.base, 2)

    def to_line(self, device, window, target, way, own):
        slot = self.slot(device)
        index = slot
        if isinstance(way, int) and way == 1:
            index = self.group // 2 + lax.rem(slot, 2)
        return self.copy(
            device, window, target, self.line.at[index], self.recv.at[slot], own
        )

    def to_side(self, device, window, target, own):
        index = lax.div(device - self.base, GROUP1) if self.side.shape[0] > 1 else 0
        slot = self.slot(device)
        return self.copy(device, window, target, self.side.at[index], self.recv.at[slot], own)

    def to_core(self, device, window, target, own):
        return self.copy(device, window, target, self.core.at[0], self.recv_core.at[0], own)

    def arrived(self, device, window):
        self.to_line(device, window, self.me, 0, False).wait_recv()

    def all_core(self):
        return pltpu.make_async_remote_copy(
            src_ref=self.total,
            dst_ref=self.total,
            send_sem=self.core.at[0],
            recv_sem=self.recv_core.at[0],
            device_id={"leaf": self.me},
            device_id_type=MESH,
        )

    def keep(self, window):
        return pltpu.make_async_copy(
            self.view(self.own, window),
            self.view(self.place(self.me - self.base), window),
            self.local.at[0],
        )


def start(copy):
    copy.start()


def wait_send(copy):
    copy.wait_send()


def dinv_of(block, cols):
    half = cols // 2
    top = block[:half]
    low = jnp.concatenate([top[:, half:].T, block[half:, half:]], axis=1)
    return jnp.concatenate([top, low], axis=0)


def solve_all(cols, lcats, jobs, after=None):
    row_ids = lax.broadcasted_iota(jnp.int32, (cols, cols), 0)
    lane_ids = lax.broadcasted_iota(jnp.int32, (cols, cols), 1)
    for i, (blocks, lhat, dinv, used, put_coup, put_diag, put) in enumerate(jobs):
        for r in range(SLOTS):
            high, low = split(jnp.where(lane_ids < used, lhat(r), 0.0))
            for part, value in enumerate((high, low, high)):
                first = (3 * r + part) * cols
                lcats[i, first : first + cols] = value
    turned = [[] for _ in jobs]
    for r in range(SLOTS):
        for i, (blocks, lhat, dinv, used, put_coup, put_diag, put) in enumerate(jobs):
            parts = []
            for k in range(SLOTS):
                high, low = blocks(r, k)
                parts += [high, high, low]
            wide = jnp.concatenate(parts, axis=1)
            coup = -jnp.dot(wide, lcats[i], preferred_element_type=f32)
            put_coup(r, coup)
            high, low = split(coup)
            high_t, low_t = high.T, low.T
            if put is not None:
                put(1 + r, high, low)
                put(1 + SLOTS + r, high_t, low_t)
            turned[i] += [high_t, high_t, low_t]
        if after is not None:
            after(r)
    for i, (blocks, lhat, dinv, used, put_coup, put_diag, put) in enumerate(jobs):
        wide = jnp.concatenate(turned[i], axis=1)
        product = jnp.dot(wide, lcats[i], preferred_element_type=f32)
        keep = (lane_ids < used) & (row_ids < used)
        diag = jnp.where(keep, dinv(), 0.0) - product
        put_diag(diag)
        if put is not None:
            put(0, *split(diag))


def gather_kernel(
    n,
    columns_in,
    pattern_in,
    root_in,
    tl_in,
    td_in,
    ml_in,
    md_in,
    pool_h,
    pool_l,
    top_coup_out,
    top_diag_out,
    ml_all,
    md_all,
    root_all,
    tl_all,
    td_all,
    top_c,
    top_d,
    lcats,
    columns,
    pattern,
    small_sems,
    *sems,
):
    me = lax.axis_index("leaf")
    core = lax.rem(me, 2)
    side = lax.rem(lax.div(me, 2), 2)
    cpeer = me + 1 - 2 * core
    xpeer = me + 2 - 4 * side
    other = cpeer + xpeer - me
    cols = td_in.shape[1]
    frame = SLOTS * cols
    half = cols // 2
    per = root_in.shape[1] // cols

    def rows_of(ref, rows):
        return lambda slot: ref.at[pl.ds(pl.multiple_of(slot * rows, 8), rows)]

    def next_sems():
        nonlocal sems
        taken, sems = sems[:6], sems[6:]
        return taken

    def by_rows(own, whole, group, windows=None):
        rows, width = own.shape
        tiles = width // TILE
        widths = [c1 - c0 for c0, c1 in windows] if windows else [tiles]
        half_of = group * rows // 2 * sum(widths) // (len(widths) * tiles)
        place = rows_of(whole, rows)
        return Part(own, place, group, next_sems(), me, whole.at[0:half_of], rows, windows)

    root = by_rows(root_in, root_all, n, root_windows(per * cols // TILE))
    tl = by_rows(tl_in, tl_all, GROUP2)
    td = by_rows(td_in, td_all, GROUP2, half_windows(cols // TILE))

    def mid_part(own, whole, *index):
        place = lambda slot: whole.at[(slot,) + index]
        total = whole.at[(slice(0, 2),) + index]
        return Part(own.at[index], place, GROUP1, next_sems(), me, total)

    cut = 2 * cols
    md0 = mid_part(md_in, md_all, slice(0, half))
    md1 = mid_part(md_in, md_all, slice(half, cols), slice(half, cols))
    ml0 = mid_part(ml_in, ml_all, slice(0, cut))
    ml1 = mid_part(ml_in, ml_all, slice(cut, frame))
    mids = (md0, md1, ml0, ml1)

    line = n // GROUP1
    place = lax.div(me, GROUP1)
    top_line = GROUP2 // GROUP1
    top_place = lax.div(lax.rem(me, GROUP2), GROUP1)
    has_next = (place < line - 1, place > 0)
    top_next = (top_place < top_line - 1, top_place > 0)

    fetches = [
        pltpu.make_async_copy(a, b, small_sems.at[i])
        for i, (a, b) in enumerate([(columns_in, columns), (pattern_in, pattern)])
    ]
    for fetch in fetches:
        fetch.start()

    barrier = pltpu.get_barrier_semaphore()

    def greet(target):
        pl.semaphore_signal(barrier, inc=1, device_id={"leaf": target}, device_id_type=MESH)

    greet(cpeer)
    greet(xpeer)
    pl.when(has_next[0])(lambda: greet(me + GROUP1))
    pl.when(has_next[1])(lambda: greet(me - GROUP1))
    both = (root, tl)
    single = (td,)
    everything = single + both + mids
    for part in everything:
        part.cases(me, lambda w, part=part: part.keep(w).start())
    peers = 2 + jnp.minimum(place, 1) + jnp.minimum(line - 1 - place, 1)
    pl.semaphore_wait(barrier, peers)

    def along(part, device, window, way, act, own=False):
        up, down = has_next if part.group == n else top_next
        if isinstance(way, int):
            ok, target = (down, me - GROUP1) if way else (up, me + GROUP1)
        else:
            ok, target = jnp.where(way == 0, up, down), me + GROUP1 - 2 * GROUP1 * way
        pl.when(ok)(lambda: act(part.to_line(device, window, target, way, own)))

    def side_to(part, device, window, act, own=False):
        act(part.to_side(device, window, xpeer, own))

    def core_to(part, device, window, act, own=False):
        if act is start:
            act(part.to_core(device, window, cpeer, own))

    def own_moves(part, act, lines=True, side=True, core=True):
        def moves(window):
            if lines:
                along(part, me, window, 0, act, True)
                along(part, me, window, 1, act, True)
            if side:
                side_to(part, me, window, act, True)
            if core:
                core_to(part, me, window, act, True)

        part.cases(me, moves)

    for part in both:
        own_moves(part, start, lines=False, core=False)
    for part in single + both:
        own_moves(part, start, side=False, core=False)
    for part in single + mids:
        own_moves(part, start, lines=False, core=False)
    for part in everything:
        own_moves(part, start, lines=False, side=False)

    def passed(part, device, way, act, side=False, wait=False):
        def moves(window):
            if wait:
                part.arrived(device, window)
            if way is None:
                along(part, device, window, 0, act)
                along(part, device, window, 1, act)
            else:
                along(part, device, window, way, act)
            if side:
                side_to(part, device, window, act)
            core_to(part, device, window, act)

        part.cases(device, moves)

    for part in both:
        passed(part, xpeer, None, start, wait=True)

    outer = lax.div(2 * place, line)

    def steps(act, wait):
        def step(s, carry):
            def turn(t, carry):
                way = lax.rem(t + 1 + outer, 2)
                shift = (2 * way - 1) * s * GROUP1
                got_top = jnp.where(way == 0, top_place >= s, top_place + s < top_line)
                got_root = jnp.where(way == 0, place >= s, place + s < line)

                @pl.when(got_top)
                def _():
                    for part in single:
                        passed(part, me + shift, way, act, side=True, wait=wait)

                def one(i, carry):
                    device = jnp.where(i == 0, me, xpeer) + shift

                    @pl.when(got_root)
                    def _():
                        passed(root, device, way, act, wait=wait)

                    @pl.when(got_top)
                    def _():
                        passed(tl, device, way, act, wait=wait)

                    return carry

                lax.fori_loop(0, 2, one, 0)
                return carry

            lax.fori_loop(0, 2, turn, 0)
            return carry

        lax.fori_loop(1, line, step, 0)

    steps(start, True)

    def crossed(part, device, act, wait):
        def moves(window):
            if wait:
                part.arrived(device, window)
            core_to(part, device, window, act)

        part.cases(device, moves)

    def tops_crossed(act, wait):
        for q in range(top_line):
            for part in single:
                crossed(part, part.base + q * GROUP1 + lax.rem(xpeer, GROUP1), act, wait)

    tops_crossed(start, True)
    for part in mids[:3]:
        crossed(part, xpeer, start, True)

    def from_core(part):
        part.all_core().wait_recv()
        part.cases(me, lambda w: part.keep(w).wait())

    from_core(root)
    tiles = cols // TILE
    windows = root.windows
    for r, (c0, c1) in enumerate(windows):
        for c in range(c0, c1):
            value = root_all[r * TILE : (r + 1) * TILE, c * TILE : (c + 1) * TILE]
            for a, b, tile in ((r, c, value), (c, r, value.T))[: 1 if r == c else 2]:
                high, low = split(tile)
                index = (a // tiles) * per + b // tiles
                rows = slice(a % tiles * TILE, (a % tiles + 1) * TILE)
                lanes = slice(b % tiles * TILE, (b % tiles + 1) * TILE)
                pool_h[index, rows, lanes] = high
                pool_l[index, rows, lanes] = low
    for fetch in fetches:
        fetch.wait()
    for part in single + (tl,):
        from_core(part)

    top_base = lax.div(me, GROUP2) * NODES2
    roots = per * per

    def top_job(q):
        chosen = [pattern[top_base + q, k] for k in range(SLOTS)]

        def blocks(r, k):
            index = chosen[r] * per + chosen[k]
            return pool_h[index], pool_l[index]

        def lhat(r):
            return tl_all[q * frame + r * cols : q * frame + (r + 1) * cols]

        def put_coup(r, value):
            top_c[q * frame + r * cols : q * frame + (r + 1) * cols] = value

        def put_diag(value):
            top_d[q * cols : (q + 1) * cols] = value

        def put(which, high, low):
            pool_h[roots + q * OWN + which] = high
            pool_l[roots + q * OWN + which] = low

        def dinv():
            return dinv_of(td_all[q * cols : (q + 1) * cols], cols)

        return blocks, lhat, dinv, columns[top_base + q], put_coup, put_diag, put

    solve_all(cols, lcats, [top_job(q) for q in range(NODES2)])
    member = lax.rem(me, GROUP2)
    rows = top_coup_out.shape[0]
    top_coup_out[...] = top_c[pl.ds(pl.multiple_of(member * rows, 8), rows)]
    rows = top_diag_out.shape[0]
    top_diag_out[...] = top_d[pl.ds(pl.multiple_of(member * rows, 8), rows)]

    crossed(ml1, xpeer, start, True)
    for part in mids:
        from_core(part)

    for part in both:
        own_moves(part, wait_send)
        passed(part, xpeer, None, wait_send)
    for part in single:
        own_moves(part, wait_send)
    for part in mids:
        own_moves(part, wait_send, lines=False)
    steps(wait_send, False)
    for part in everything:
        part.all_core().wait_send()


def tree_kernel(per, *refs):
    small_in, refs = refs[:8], refs[8:]
    pool_h, pool_l, top_coup, top_diag, ml_all, md_all, leaf_lhat_in, leaf_dinv_in = refs[:8]
    top_diag_out, top_coup_out, mid_diag_out, mid_coup_out, leaf_diag_out, leaf_coup_out = refs[8:14]
    e1h, e1l, lcats, leaf_lhat, leaf_dinv, mid_c, mid_d, leaf_c, leaf_d = refs[14:23]
    small = refs[23:31]
    in_sems, out_sems = refs[31:]
    (
        mid_columns,
        leaf_columns,
        top_pattern,
        mid_parent,
        leaf_parent,
        mid_pattern,
        leaf_pattern,
        leaf_live,
    ) = small
    fetched = list(zip(small_in + (leaf_lhat_in, leaf_dinv_in), small + (leaf_lhat, leaf_dinv)))
    fetches = [pltpu.make_async_copy(a, b, in_sems.at[i]) for i, (a, b) in enumerate(fetched)]
    for fetch in fetches:
        fetch.start()
    tops = [
        pltpu.make_async_copy(top_coup, top_coup_out, out_sems.at[0]),
        pltpu.make_async_copy(top_diag, top_diag_out, out_sems.at[1]),
    ]
    for copy in tops:
        copy.start()
    me = lax.axis_index("leaf")
    leaves, cols = leaf_dinv.shape[0], leaf_dinv.shape[2]
    roots = per * per
    top_base = lax.div(me, GROUP2) * NODES2
    mid_base = lax.div(me, GROUP1) * GROUP1
    mine = lax.rem(me, GROUP1)
    for fetch in fetches[:-2]:
        fetch.wait()
    live = leaf_live[me]

    def pool_index(node, u, v):
        parent = mid_parent[node] - top_base
        a = mid_pattern[u, node]
        b = mid_pattern[v, node]
        base = roots + parent * OWN
        near = base + jnp.where(b == 0, a, SLOTS + b)
        far_a = top_pattern[top_base + parent, jnp.maximum(a - 1, 0)]
        far_b = top_pattern[top_base + parent, jnp.maximum(b - 1, 0)]
        return jnp.where((a == 0) | (b == 0), near, far_a * per + far_b)

    parents = [leaf_parent[me * leaves + i] - mid_base for i in range(leaves)]

    def mid_job(k):
        local = parents[k - 1] if k else mine
        node = mid_base + local

        def blocks(r, c):
            index = pool_index(node, r, c)
            return pool_h[index], pool_l[index]

        def lhat(r):
            return ml_all[local, r * cols : (r + 1) * cols]

        def put_coup(r, value):
            if k == 0:
                mid_c[r * cols : (r + 1) * cols] = value

        def put_diag(value):
            if k == 0:
                mid_d[...] = value

        def put(which, high, low):
            e1h[k, which] = high
            e1l[k, which] = low

        def dinv():
            return dinv_of(md_all[local], cols)

        return blocks, lhat, dinv, mid_columns[node], put_coup, put_diag, put

    solve_all(cols, lcats, [mid_job(k) for k in range(leaves + 1)])
    outs = [
        pltpu.make_async_copy(mid_c, mid_coup_out, out_sems.at[2]),
        pltpu.make_async_copy(mid_d, mid_diag_out, out_sems.at[3]),
    ]
    for copy in outs:
        copy.start()
    for fetch in fetches[-2:]:
        fetch.wait()

    def leaf_job(i):
        node = me * leaves + i
        above = mid_base + parents[i]
        alive = jnp.full((cols, cols), i, jnp.int32) < live

        def blocks(r, c):
            if r == 0 or c == 0:
                if r == 0:
                    which = leaf_pattern[c, node] + SLOTS if c else 0
                else:
                    which = leaf_pattern[r, node]
                return e1h[i + 1, which], e1l[i + 1, which]
            index = pool_index(above, leaf_pattern[r, node] - 1, leaf_pattern[c, node] - 1)
            return pool_h[index], pool_l[index]

        def lhat(r):
            return leaf_lhat[i, r * cols : (r + 1) * cols]

        def put_coup(r, value):
            leaf_c[i, r * cols : (r + 1) * cols] = jnp.where(alive, value, 0.0)

        def put_diag(value):
            leaf_d[i] = jnp.where(alive, value, 0.0)

        def dinv():
            return leaf_dinv[i]

        return blocks, lhat, dinv, leaf_columns[node], put_coup, put_diag, None

    def leaf_rows(r):
        for i in range(leaves):
            rows = pl.ds(r * cols, cols)
            copy = pltpu.make_async_copy(
                leaf_c.at[i, rows],
                leaf_coup_out.at[i, rows],
                out_sems.at[4 + i * (SLOTS + 1) + r],
            )
            copy.start()
            outs.append(copy)

    def after(r):
        if r:
            leaf_rows(r - 1)

    solve_all(cols, lcats, [leaf_job(i) for i in range(leaves)], after)
    leaf_rows(SLOTS - 1)
    for i in range(leaves):
        copy = pltpu.make_async_copy(
            leaf_d.at[i], leaf_diag_out.at[i], out_sems.at[4 + i * (SLOTS + 1) + SLOTS]
        )
        copy.start()
        outs.append(copy)
    for copy in tops + outs:
        copy.wait()


def body(
    root_frame,
    top_lhat,
    top_dinv,
    mid_lhat,
    mid_dinv,
    leaf_lhat,
    leaf_dinv,
    top_columns,
    mid_columns,
    leaf_columns,
    top_pattern,
    mid_parent,
    leaf_parent,
    mid_pattern,
    leaf_pattern,
    leaf_live,
):
    n = lax.axis_size("leaf")
    cols = top_dinv.shape[1]
    frame = SLOTS * cols
    per = root_frame.shape[1] // cols
    leaves = leaf_lhat.shape[0]
    pool = per * per + NODES2 * OWN

    def dma(count):
        return pltpu.SemaphoreType.DMA((count,))

    def part_sems(group, line, side):
        return [dma(group // 2), dma(1), dma(line), dma(side), dma(1), dma(1)]

    sems = part_sems(n, n // 2 + 2, 1) + part_sems(GROUP2, GROUP2 // 2 + 2, 1)
    sems += part_sems(GROUP2, GROUP2 // 2 + 2, GROUP2 // GROUP1)
    for _ in range(4):
        sems += part_sems(GROUP1, 1, 1)
    vmem = pl.BlockSpec(memory_space=pltpu.VMEM)
    hbm = pl.BlockSpec(memory_space=pltpu.HBM)
    shape = jax.ShapeDtypeStruct
    moved = (top_columns, top_pattern, root_frame, top_lhat, top_dinv, mid_lhat[0], mid_dinv[0])
    pool_h, pool_l, top_coup, top_diag, ml_all, md_all = pl.pallas_call(
        functools.partial(gather_kernel, n),
        out_shape=[
            shape((pool, cols, cols), bf16),
            shape((pool, cols, cols), bf16),
            shape(top_lhat.shape, f32),
            shape(top_dinv.shape, f32),
            shape((GROUP1, frame, cols), f32),
            shape((GROUP1, cols, cols), f32),
        ],
        in_specs=[hbm] * 7,
        out_specs=[vmem] * 6,
        scratch_shapes=[
            pltpu.VMEM((per * cols, per * cols), f32),
            pltpu.VMEM((NODES2 * frame, cols), f32),
            pltpu.VMEM((NODES2 * cols, cols), f32),
            pltpu.VMEM((NODES2 * frame, cols), f32),
            pltpu.VMEM((NODES2 * cols, cols), f32),
            pltpu.VMEM((NODES2, 3 * frame, cols), bf16),
            pltpu.SMEM(top_columns.shape, jnp.int32),
            pltpu.SMEM(top_pattern.shape, jnp.int32),
            dma(2),
        ]
        + sems,
        compiler_params=pltpu.CompilerParams(
            collective_id=0, has_side_effects=True, vmem_limit_bytes=20 * 1024 * 1024
        ),
    )(*[in_hbm(x) for x in moved])
    small = (
        mid_columns,
        leaf_columns,
        top_pattern,
        mid_parent,
        leaf_parent,
        mid_pattern.T,
        leaf_pattern.T,
        leaf_live,
    )
    outs = pl.pallas_call(
        functools.partial(tree_kernel, per),
        out_shape=[
            shape(top_dinv.shape, f32),
            shape(top_lhat.shape, f32),
            shape(mid_dinv.shape[1:], f32),
            shape(mid_lhat.shape[1:], f32),
            shape(leaf_dinv.shape, f32),
            shape(leaf_lhat.shape, f32),
        ],
        in_specs=[hbm] * 8 + [vmem] * 6 + [hbm] * 2,
        out_specs=[hbm] * 6,
        scratch_shapes=[
            pltpu.VMEM((leaves + 1, OWN, cols, cols), bf16),
            pltpu.VMEM((leaves + 1, OWN, cols, cols), bf16),
            pltpu.VMEM((leaves + 1, 3 * frame, cols), bf16),
            pltpu.VMEM(leaf_lhat.shape, f32),
            pltpu.VMEM(leaf_dinv.shape, f32),
            pltpu.VMEM((frame, cols), f32),
            pltpu.VMEM((cols, cols), f32),
            pltpu.VMEM(leaf_lhat.shape, f32),
            pltpu.VMEM(leaf_dinv.shape, f32),
        ]
        + [pltpu.SMEM(x.shape, jnp.int32) for x in small]
        + [dma(len(small) + 2), dma(4 + leaves * (SLOTS + 1))],
        compiler_params=pltpu.CompilerParams(vmem_limit_bytes=24 * 1024 * 1024),
    )(
        *[in_hbm(x) for x in small],
        pool_h,
        pool_l,
        top_coup,
        top_diag,
        ml_all,
        md_all,
        in_hbm(leaf_lhat),
        in_hbm(leaf_dinv),
    )
    return (outs[0], outs[1], outs[2][None], outs[3][None], outs[4], outs[5])


def solution(mesh):
    rows = P(("pole", "leaf"), None)
    stacks = P(("pole", "leaf"), None, None)
    in_specs = (rows,) * 3 + (stacks,) * 4 + (P(),) * 9
    out_specs = (rows,) * 2 + (stacks,) * 4
    return jax.shard_map(body, mesh=mesh, in_specs=in_specs, out_specs=out_specs, check_vma=False)
```

time: 71.4 us -> 54 us (0.76)
  Pallas kernels: 69 us -> 53.2 us
  local copies, waits for them, and re-layouts: 1.52 us -> 0 us
    pallas_call x2, Pallas kernels: 69 us -> 53.2 us  [the longest x1 44.8 us: body(): pl.pallas_call(functools.partial(gather_kernel, n), out_shape=[shape((poo...]
    unnamed x2 -> x0, local copies, waits for them, and re-layouts: 1.52 us -> none
where the time goes in v1:
time: 54 us; the launch traced here: 53.8 us
  Pallas kernels  53.2 us (99%)
  between operations  0.64 us (1%)
    pallas_call x1, Pallas kernels, body(): pl.pallas_call(functools.partial(gather_kernel, n), out_shape=[shape((poo...  44.8 us
    pallas_call x1, Pallas kernels, body(): pl.pallas_call(functools.partial(tree_kernel, per), out_shape=[shape(top_...  8.41 us

profile of v1, /device:TPU:0, one launch (start us, length us, event | category | flops | bytes accessed | tf_op | source)
XLA Modules:
  0.0 53.8 jit_solution(8795767547773381077)
XLA Ops:
  0.6 44.8 %shard_map.199 = (bf16[30,256,256]{2,1,0:T(8,128)(2,1)S(1)}, bf16[30,256,256]{2,1,0:T(8,128)(2,1)S(1)}, f32[96,256]{1,0:T(8,128)S(1)}, f32[32,256]{1,0:T(8,128)S...) custom-call(s32[2]{0:T(128)} %columns_in.1, s32[2,3]{1,0:T(2,128)} %refs_2_.1, f32[64,1024]{1,0:T(8,128)} %root_in.1, ...), custom_call_target="tpu_custom_call" | custom-call | tf_op jit(solution)/shard_map/pallas_call | solution.py:631
  45.4 8.4 %shard_map.200 = (f32[32,256]{1,0:T(8,128)}, f32[96,256]{1,0:T(8,128)}, f32[256,256]{1,0:T(8,128)}, f32[768,256]{1,0:T(8,128)}, f32[2,256,256]{2,1,0:T(8,128)}, /*index=5*/f32[2,768,256]{2,1,0:T(8,128)}) custom-call(s32[16]{0:T(128)} %refs_0_.1, s32[32]{0:T(128)} %refs_1_.1, s32[2,3]{1,0:T(2,128)} %refs_2_.1, s32[16]{0:T(128)} %refs_3_.1, s32[32]{0:T(128)} %refs_4_.1, ...), custom_call_target="tpu_custom_call" | custom-call | tf_op jit(solution)/shard_map/pallas_call | solution.py:669

commit v2 on v1

--- a/solution.py
+++ b/solution.py
@@ -201,24 +201,28 @@
     half = cols // 2
     per = root_in.shape[1] // cols
 
-    def rows_of(ref, rows):
-        return lambda slot: ref.at[pl.ds(pl.multiple_of(slot * rows, 8), rows)]
+    def rows_of(ref, rows, first, count):
+        return lambda slot: ref.at[pl.ds(pl.multiple_of(slot * rows + first, 8), count)]
 
     def next_sems():
         nonlocal sems
         taken, sems = sems[:6], sems[6:]
         return taken
 
-    def by_rows(own, whole, group, windows=None):
+    def by_rows(own, whole, group, windows=None, first=0, last=None):
         rows, width = own.shape
+        count = (rows if last is None else last) - first
         tiles = width // TILE
         widths = [c1 - c0 for c0, c1 in windows] if windows else [tiles]
-        half_of = group * rows // 2 * sum(widths) // (len(widths) * tiles)
-        place = rows_of(whole, rows)
+        half_of = group * count // 2 * sum(widths) // (len(widths) * tiles)
+        place = rows_of(whole, rows, first, count)
+        own = own.at[pl.ds(first, count)]
         return Part(own, place, group, next_sems(), me, whole.at[0:half_of], rows, windows)
 
     root = by_rows(root_in, root_all, n, root_windows(per * cols // TILE))
-    tl = by_rows(tl_in, tl_all, GROUP2)
+    middle = tl_in.shape[0] // 2 // 8 * 8
+    tl = by_rows(tl_in, tl_all, GROUP2, None, 0, middle)
+    tl_side = by_rows(tl_in, tl_all, GROUP2, None, middle)
     td = by_rows(td_in, td_all, GROUP2, half_windows(cols // TILE))
 
     def mid_part(own, whole, *index):
@@ -226,12 +230,10 @@
         total = whole.at[(slice(0, 2),) + index]
         return Part(own.at[index], place, GROUP1, next_sems(), me, total)
 
-    cut = 2 * cols
     md0 = mid_part(md_in, md_all, slice(0, half))
     md1 = mid_part(md_in, md_all, slice(half, cols), slice(half, cols))
-    ml0 = mid_part(ml_in, ml_all, slice(0, cut))
-    ml1 = mid_part(ml_in, ml_all, slice(cut, frame))
-    mids = (md0, md1, ml0, ml1)
+    mls = [mid_part(ml_in, ml_all, slice(r * cols, (r + 1) * cols)) for r in range(SLOTS)]
+    mids = (md0, md1) + tuple(mls)
 
     line = n // GROUP1
     place = lax.div(me, GROUP1)
@@ -257,7 +259,7 @@
     pl.when(has_next[0])(lambda: greet(me + GROUP1))
     pl.when(has_next[1])(lambda: greet(me - GROUP1))
     both = (root, tl)
-    single = (td,)
+    single = (td, tl_side)
     everything = single + both + mids
     for part in everything:
         part.cases(me, lambda w, part=part: part.keep(w).start())
@@ -295,7 +297,7 @@
         own_moves(part, start, lines=False, core=False)
     for part in single + both:
         own_moves(part, start, side=False, core=False)
-    for part in single + mids:
+    for part in single + mids[:3]:
         own_moves(part, start, lines=False, core=False)
     for part in everything:
         own_moves(part, start, lines=False, side=False)
@@ -320,19 +322,36 @@
 
     outer = lax.div(2 * place, line)
 
+    last_step = jnp.maximum(top_place, top_line - 1 - top_place)
+
     def steps(act, wait):
         def step(s, carry):
-            def turn(t, carry):
+            def turned(t):
                 way = lax.rem(t + 1 + outer, 2)
                 shift = (2 * way - 1) * s * GROUP1
                 got_top = jnp.where(way == 0, top_place >= s, top_place + s < top_line)
                 got_root = jnp.where(way == 0, place >= s, place + s < line)
+                return way, shift, got_top, got_root
+
+            def crossing(t, carry):
+                way, shift, got_top, _ = turned(t)
 
                 @pl.when(got_top)
                 def _():
                     for part in single:
                         passed(part, me + shift, way, act, side=True, wait=wait)
 
+                return carry
+
+            lax.fori_loop(0, 2, crossing, 0)
+            if wait:
+                @pl.when(s == last_step)
+                def _():
+                    own_moves(mls[2], start, lines=False, core=False)
+
+            def turn(t, carry):
+                way, shift, got_top, got_root = turned(t)
+
                 def one(i, carry):
                     device = jnp.where(i == 0, me, xpeer) + shift
 
@@ -350,6 +369,11 @@
                 return carry
 
             lax.fori_loop(0, 2, turn, 0)
+            if wait:
+                @pl.when(s == 1)
+                def _():
+                    own_moves(mls[1], start, lines=False, core=False)
+
             return carry
 
         lax.fori_loop(1, line, step, 0)
@@ -370,7 +394,7 @@
                 crossed(part, part.base + q * GROUP1 + lax.rem(xpeer, GROUP1), act, wait)
 
     tops_crossed(start, True)
-    for part in mids[:3]:
+    for part in mids[:4]:
         crossed(part, xpeer, start, True)
 
     def from_core(part):
@@ -430,10 +454,7 @@
     rows = top_diag_out.shape[0]
     top_diag_out[...] = top_d[pl.ds(pl.multiple_of(member * rows, 8), rows)]
 
-    crossed(ml1, xpeer, start, True)
-    for part in mids:
-        from_core(part)
-
+    crossed(mls[2], xpeer, start, True)
     for part in both:
         own_moves(part, wait_send)
         passed(part, xpeer, None, wait_send)
@@ -442,6 +463,8 @@
     for part in mids:
         own_moves(part, wait_send, lines=False)
     steps(wait_send, False)
+    for part in mids:
+        from_core(part)
     for part in everything:
         part.all_core().wait_send()
 
@@ -621,8 +644,9 @@
         return [dma(group // 2), dma(1), dma(line), dma(side), dma(1), dma(1)]
 
     sems = part_sems(n, n // 2 + 2, 1) + part_sems(GROUP2, GROUP2 // 2 + 2, 1)
-    sems += part_sems(GROUP2, GROUP2 // 2 + 2, GROUP2 // GROUP1)
-    for _ in range(4):
+    for _ in range(2):
+        sems += part_sems(GROUP2, GROUP2 // 2 + 2, GROUP2 // GROUP1)
+    for _ in range(2 + SLOTS):
         sems += part_sems(GROUP1, 1, 1)
     vmem = pl.BlockSpec(memory_space=pltpu.VMEM)
     hbm = pl.BlockSpec(memory_space=pltpu.HBM)

time: 54 us -> 51.3 us (0.950)
  Pallas kernels: 53.2 us -> 50.6 us
    pallas_call x1, Pallas kernels: 44.8 us -> 42.2 us  [body(): pl.pallas_call(functools.partial(gather_kernel, n), out_shape=[shape((poo...]
where the time goes in v2:
time: 51.3 us; the launch traced here: 51.2 us
  Pallas kernels  50.6 us (99%)
  between operations  0.64 us (1%)
    pallas_call x1, Pallas kernels, body(): pl.pallas_call(functools.partial(gather_kernel, n), out_shape=[shape((poo...  42.2 us
    pallas_call x1, Pallas kernels, body(): pl.pallas_call(functools.partial(tree_kernel, per), out_shape=[shape(top_...  8.4 us

profile of v2, /device:TPU:0, one launch (start us, length us, event | category | flops | bytes accessed | tf_op | source)
XLA Modules:
  0.0 51.2 jit_solution(15498666161565919028)
XLA Ops:
  0.6 42.2 %shard_map.199 = (bf16[30,256,256]{2,1,0:T(8,128)(2,1)S(1)}, bf16[30,256,256]{2,1,0:T(8,128)(2,1)S(1)}, f32[96,256]{1,0:T(8,128)S(1)}, f32[32,256]{1,0:T(8,128)S...) custom-call(s32[2]{0:T(128)} %columns_in.1, s32[2,3]{1,0:T(2,128)} %refs_2_.1, f32[64,1024]{1,0:T(8,128)} %root_in.1, ...), custom_call_target="tpu_custom_call" | custom-call | tf_op jit(solution)/shard_map/pallas_call | solution.py:655
  42.8 8.4 %shard_map.200 = (f32[32,256]{1,0:T(8,128)}, f32[96,256]{1,0:T(8,128)}, f32[256,256]{1,0:T(8,128)}, f32[768,256]{1,0:T(8,128)}, f32[2,256,256]{2,1,0:T(8,128)}, /*index=5*/f32[2,768,256]{2,1,0:T(8,128)}) custom-call(s32[16]{0:T(128)} %refs_0_.1, s32[32]{0:T(128)} %refs_1_.1, s32[2,3]{1,0:T(2,128)} %refs_2_.1, s32[16]{0:T(128)} %refs_3_.1, s32[32]{0:T(128)} %refs_4_.1, ...), custom_call_target="tpu_custom_call" | custom-call | tf_op jit(solution)/shard_map/pallas_call | solution.py:693

commit v3 on v2

--- a/solution.py
+++ b/solution.py
@@ -31,7 +31,7 @@
 
 def root_windows(tiles):
     if tiles == 8:
-        return [(0, 7), (1, 7), (2, 6), (3, 6), (4, 6), (5, 6), (2, 7), (0, 8)]
+        return [(0, 8), (1, 7), (2, 6), (3, 6), (4, 6), (5, 6), (2, 7), (1, 8)]
     return [(r, tiles) for r in range(tiles)]
 
 

time: 51.3 us -> 51.4 us (level)
  no operation moved by 1% of the time
where the time goes in v3:
time: 51.4 us; the launch traced here: 51.2 us
  Pallas kernels  50.6 us (98%)
  between operations  0.64 us (1%)
    pallas_call x1, Pallas kernels, body(): pl.pallas_call(functools.partial(gather_kernel, n), out_shape=[shape((poo...  42.2 us
    pallas_call x1, Pallas kernels, body(): pl.pallas_call(functools.partial(tree_kernel, per), out_shape=[shape(top_...  8.4 us

profile of v3, /device:TPU:0, one launch (start us, length us, event | category | flops | bytes accessed | tf_op | source)
XLA Modules:
  0.0 51.2 jit_solution(5455387549868521007)
XLA Ops:
  0.6 42.2 %shard_map.199 = (bf16[30,256,256]{2,1,0:T(8,128)(2,1)S(1)}, bf16[30,256,256]{2,1,0:T(8,128)(2,1)S(1)}, f32[96,256]{1,0:T(8,128)S(1)}, f32[32,256]{1,0:T(8,128)S...) custom-call(s32[2]{0:T(128)} %columns_in.1, s32[2,3]{1,0:T(2,128)} %refs_2_.1, f32[64,1024]{1,0:T(8,128)} %root_in.1, ...), custom_call_target="tpu_custom_call" | custom-call | tf_op jit(solution)/shard_map/pallas_call | solution.py:655
  42.8 8.4 %shard_map.200 = (f32[32,256]{1,0:T(8,128)}, f32[96,256]{1,0:T(8,128)}, f32[256,256]{1,0:T(8,128)}, f32[768,256]{1,0:T(8,128)}, f32[2,256,256]{2,1,0:T(8,128)}, /*index=5*/f32[2,768,256]{2,1,0:T(8,128)}) custom-call(s32[16]{0:T(128)} %refs_0_.1, s32[32]{0:T(128)} %refs_1_.1, s32[2,3]{1,0:T(2,128)} %refs_2_.1, s32[16]{0:T(128)} %refs_3_.1, s32[32]{0:T(128)} %refs_4_.1, ...), custom_call_target="tpu_custom_call" | custom-call | tf_op jit(solution)/shard_map/pallas_call | solution.py:693
